TPU v7x, 32 devices: a whole 2x2x4 slice. The times are simulated.
32 devices in a mesh: shard: 32 (over z, y, x, core).
Axes of the slice: x: 2, y: 2, z: 4, core: 2. Of those that a mesh axis runs over, the one named last changes fastest.
Arguments:
- data_t: bfloat16 [8192, 8192], P('shard'), may hold values from -0.125 to 0.125
- labels: int32 [8192], replicated, may hold values from -1 to 1, as said below
- sample_weight: float32 [8192], replicated, may hold values from 0.1 to 4
- w_start: float32 [8192], P('shard'), may hold values from -10 to 10
- alpha_start: float32 [8192], P('shard'), may hold values from 0 to 1
- visit_order: int32 [64, 128], P('shard'), may hold values from 0 to 127, each once within a row
Outputs:
- weights_out: float32 [8192], P('shard')
- alpha_final: float32 [8192], P('shard')
- objective: float32 [], replicated
Inputs may be any that keep to these rules, and one draw needn't show every extreme that they name: `labels`: each label is -1 or +1. `visit_order`: each row is a permutation of 0 to 127.
All inputs are finite; a program needn't handle non-finite values.
Results may differ from a plain program's by a relative error of at most 0.0047.
Values may be sent and summed in bfloat16 or wider, within the bound.
A program may use at most 64 MiB of HBM per device.

v0:
```python
import jax
import jax.numpy as jnp
from jax import lax
from jax.sharding import PartitionSpec as P

GROUP = 16


def sweep_rows(gram_block, label_rows, bound_rows, alpha_rows, margin_rows, visit_rows):
    gram_perm = gram_block[visit_rows][:, visit_rows]
    label_perm = label_rows[visit_rows]
    bound_perm = bound_rows[visit_rows]
    alpha_perm = alpha_rows[visit_rows]
    margin_perm = margin_rows[visit_rows]
    diag_perm = jnp.diagonal(gram_perm) + 1e-06

    def update_group(group_index, state_pair):
        alpha_now, margin_now = state_pair
        first_row = jnp.asarray(group_index * GROUP).astype(jnp.int32)
        group_alpha = lax.dynamic_slice_in_dim(alpha_now, first_row, GROUP)
        group_label = lax.dynamic_slice_in_dim(label_perm, first_row, GROUP)
        group_margin = lax.dynamic_slice_in_dim(margin_now, first_row, GROUP)
        group_diag = lax.dynamic_slice_in_dim(diag_perm, first_row, GROUP)
        group_bound = lax.dynamic_slice_in_dim(bound_perm, first_row, GROUP)
        fresh_alpha = jnp.clip(
            group_alpha + (1.0 - group_label * group_margin) / (2.0 * group_diag), 0.0, group_bound
        )
        change = fresh_alpha - group_alpha
        columns = lax.dynamic_slice_in_dim(gram_perm, first_row, GROUP, 1)
        margin_now = margin_now + 2.0 * jnp.dot(
            columns, group_label * change, precision=lax.Precision.HIGHEST
        )
        alpha_now = lax.dynamic_update_slice_in_dim(alpha_now, fresh_alpha, first_row, 0)
        return (alpha_now, margin_now)

    alpha_perm, margin_perm = lax.fori_loop(
        0, alpha_rows.shape[0] // GROUP, update_group, (alpha_perm, margin_perm)
    )
    return jnp.zeros_like(alpha_rows).at[visit_rows].set(alpha_perm)


def body(data_t, labels, sample_weight, w_start, alpha_start, visit_order):
    device_index = lax.axis_index("shard")
    devices = lax.axis_size("shard")
    local_feat = data_t.shape[0]
    samples = labels.shape[0]
    row_count = alpha_start.shape[0]
    features = local_feat * devices
    label_sign = labels.astype(jnp.float32)
    row_first = device_index * row_count
    own_signs = lax.dynamic_slice_in_dim(label_sign, row_first, row_count)
    own_bound = lax.dynamic_slice_in_dim(sample_weight, row_first, row_count)
    relaid = lax.all_to_all(data_t, "shard", split_axis=1, concat_axis=0, tiled=True)
    start_part = jnp.dot(w_start.astype(jnp.bfloat16), data_t, preferred_element_type=jnp.float32)
    start_margin = lax.psum(start_part, "shard")
    weighted = (
        sample_weight * label_sign * jnp.maximum(0.0, 1.0 - label_sign * start_margin)
    ).astype(jnp.bfloat16)
    ascent = jnp.dot(data_t, weighted, preferred_element_type=jnp.float32)
    column_sq = jnp.einsum("fs,fs->f", data_t, data_t, preferred_element_type=jnp.float32)
    scale_col = column_sq / samples + 1e-06
    stepped = w_start + ascent / (samples * scale_col)
    thresh = 1.0 / (4.0 * features * scale_col)
    primal = stepped - jnp.clip(stepped, -thresh, thresh)
    model_part = jnp.dot(primal.astype(jnp.bfloat16), data_t, preferred_element_type=jnp.float32)
    penalty_part = jnp.sum(jnp.abs(primal)) / (4.0 * features)
    own_margin = lax.psum_scatter(model_part, "shard", scatter_dimension=0, tiled=True)
    loss_part = jnp.sum(own_bound * jnp.square(jnp.maximum(0.0, 1.0 - own_signs * own_margin))) / (
        2.0 * samples
    )
    loss_total, penalty = lax.psum((loss_part, penalty_part), "shard")
    objective = loss_total + penalty
    gram_block = lax.dot_general(
        relaid, relaid, (((0,), (0,)), ((), ())), preferred_element_type=jnp.float32
    )
    block_count = visit_order.shape[0]
    visit_rows = (
        visit_order + (jnp.arange(block_count, dtype=jnp.int32) * visit_order.shape[1])[:, None]
    ).reshape(row_count)
    alpha_zero = own_bound * alpha_start
    alpha_one = sweep_rows(gram_block, own_signs, own_bound, alpha_zero, own_margin, visit_rows)
    change_one = (own_signs * (alpha_one - alpha_zero)).astype(jnp.bfloat16)
    update_part = jnp.dot(relaid, change_one, preferred_element_type=jnp.float32) * (2.0 / devices)
    update_one = lax.psum(update_part, "shard")
    second_margin = own_margin + jnp.dot(
        update_one.astype(jnp.bfloat16), relaid, preferred_element_type=jnp.float32
    )
    alpha_two = sweep_rows(gram_block, own_signs, own_bound, alpha_one, second_margin, visit_rows)
    change_two = (own_signs * (alpha_two - alpha_one)).astype(jnp.bfloat16)
    second_part = jnp.dot(relaid, change_two, preferred_element_type=jnp.float32) * (2.0 / devices)
    feat_first = device_index * local_feat
    update_two = lax.psum(second_part, "shard")
    own_two = lax.dynamic_slice_in_dim(update_two, feat_first, local_feat)
    own_one = lax.dynamic_slice_in_dim(update_one, feat_first, local_feat)
    return (primal + own_one + own_two, alpha_two, objective)


def solution(mesh):
    placed = (P("shard", None), P(), P(), P("shard"), P("shard"), P("shard", None))
    return jax.shard_map(
        body, mesh=mesh, in_specs=placed, out_specs=(P("shard"), P("shard"), P()), check_vma=False
    )
```

profile of v0, /device:TPU:14, one launch (start us, length us, event | category | flops | bytes accessed | tf_op | source)
XLA Modules:
  0.0 315.5 jit_solution(12440864550533348112)
XLA Ops:
  0.6 6.4 %copy.19 = bf16[256,8192]{0,1:T(8,128)(2,1)} copy(bf16[256,8192]{1,0:T(8,128)(2,1)} %param.10) | data formatting | bytes 8388608 | tf_op args[0]
  7.0 6.4 %copy.20 = bf16[256,32,256]{2,0,1:T(8,128)(2,1)} copy(bf16[256,32,256]{0,2,1:T(8,128)(2,1)} %bitcast.48) | data formatting | bytes 8388608 | tf_op jit(solution)/shard_map/all_to_all | solution.py:53
  13.4 6.0 %all-to-all-start = ((bf16[256,32,256]{2,0,1:T(8,128)(2,1)}), bf16[256,32,256]{2,0,1:T(8,128)(2,1)}, u32[]{:S(2)}, u32[]{:S(2)}) async-start(bf16[256,32,256]{2,0,1:T(8,128)(2,1)} %copy.20), calls=%async_computation | async-start | bytes 8388608 | tf_op jit(solution)/shard_map/all_to_all | solution.py:53
  19.5 2.8 fusion.28
  22.4 109.1 %psum.35 = f32[8192]{0:T(1024)S(1)} all-reduce(f32[8192]{0:T(1024)S(1)} %bitcast.53), channel_id=1, replica_groups=mesh['shard'=32] {'shard'}, use_global_device_ids=true, to_apply=%region_0.0 | all-reduce | flops 8192 | bytes 65536 | tf_op jit(solution)/shard_map/psum | solution.py:55
  131.5 3.5 %fusion.29 = f32[1,256]{1,0:T(1,128)S(1)} fusion(bf16[8192,1]{0,1:T(2,128)(2,1)S(1)} %reshape.137, bf16[256,8192]{1,0:T(8,128)(2,1)} %param.10), kind=kOutput, calls=%fused_computation.58 | convolution fusion | flops 4194304 | bytes 4211712 | tf_op jit(solution)/shard_map/dot_general | solution.py:59
  136.6 2.8 fusion.30
  139.5 42.1 %all-reduce = f32[8192]{0:T(1024)S(1)} all-reduce(f32[8192]{0:T(1024)S(1)} %bitcast.54), channel_id=2, replica_groups=mesh['shard'=32] {'shard'}, use_global_device_ids=true, to_apply=%region_1.2.clone | all-reduce | flops 8192 | bytes 65536
  182.3 1.9 gather_fusion.3
  184.3 1.9 gather_fusion.2
  186.3 1.9 gather_fusion
  188.2 1.9 gather_fusion.1
  191.5 4.7 %fusion.19 = f32[256,256]{1,0:T(8,128)S(1)} fusion(bf16[256,32,256]{2,0,1:T(8,128)(2,1)} %all-to-all-done), kind=kOutput, calls=%fused_computation.35 | convolution fusion | flops 1073741824 | bytes 4456448 | tf_op jit(solution)/shard_map/dot_general | solution.py:73
  198.5 2.4 gather_fusion.6
  200.8 8.5 %while.30 = (s32[]{:T(128)}, f32[256]{0:T(256)S(1)}, f32[256]{0:T(256)S(1)}, f32[256]{0:T(256)S(1)}, f32[256]{0:T(256)S(1)}, /*index=5*/f32[256]{0:T(256)S(1)}, ...) while((s32[]{:T(128)}, f32[256]{0:T(256)S(1)}, f32[256]{0:T(256)S(1)}, ...), condition=%wide.region_3.4_spmd, body=%wide.region_2.3_spmd.sunk | while | flops 49814 | bytes 145567 | solution.py:36
  210.7 1.9 gather_fusion.7
  212.7 3.4 %fusion.31 = f32[1,8192]{1,0:T(1,128)S(1)} fusion(bf16[256,1]{0,1:T(2,128)(2,1)S(1)} %reshape.144, bf16[8192,256]{1,0:T(8,128)(2,1)} %bitcast.14), kind=kOutput, calls=%fused_computation.60 | convolution fusion | flops 4194304 | bytes 4227584 | tf_op jit(solution)/shard_map/dot_general | solution.py:83
  216.1 38.4 %psum.36 = f32[8192]{0:T(1024)S(1)} all-reduce(f32[8192]{0:T(1024)S(1)} %broadcast_multiply_fusion.1), channel_id=1, replica_groups=mesh['shard'=32] {'shard'}, use_global_device_ids=true, to_apply=%region_5.6 | all-reduce | flops 8192 | bytes 65536 | tf_op jit(solution)/shard_map/psum | solution.py:84
  254.5 2.8 fusion.32
  257.4 2.0 gather_fusion.8
  259.3 8.5 %while.31 = (s32[]{:T(128)}, f32[256]{0:T(256)S(1)}, f32[256]{0:T(256)S(1)}, f32[256]{0:T(256)S(1)}, f32[256]{0:T(256)S(1)}, /*index=5*/f32[256]{0:T(256)S(1)}, ...) while((s32[]{:T(128)}, f32[256]{0:T(256)S(1)}, f32[256]{0:T(256)S(1)}, ...), condition=%wide.region_7.8_spmd, body=%wide.region_6.7_spmd.sunk | while | flops 49814 | bytes 145567 | solution.py:36
  267.8 1.4 scatter_custom_fusion.1
  269.2 3.4 %fusion.33 = f32[1,8192]{1,0:T(1,128)S(1)} fusion(bf16[256,1]{0,1:T(2,128)(2,1)S(1)} %reshape.148, bf16[8192,256]{1,0:T(8,128)(2,1)} %bitcast.14), kind=kOutput, calls=%fused_computation.62 | convolution fusion | flops 4194304 | bytes 4227584 | tf_op jit(solution)/shard_map/dot_general | solution.py:90
  272.6 42.2 %all-reduce.1 = (f32[8192]{0:T(1024)S(1)}, f32[]{:T(128)}) all-reduce(f32[8192]{0:T(1024)S(1)} %broadcast_multiply_fusion, f32[]{:T(128)S(6)} %add.173), channel_id=1, replica_groups=mesh['shard'=32] {'shard'}, use_global_device_ids=true, to_apply=%region_9.10 | all-reduce | flops 8193 | bytes 65544 | tf_op jit(solution)/shard_map/psum | solution.py:92
  (207 shorter events, 22.2 us)
Async XLA Ops:
  13.4 6.1 %copy-start.6 = (f32[256]{0:T(256)S(1)}, f32[256]{0:T(256)}, u32[]{:S(2)}) copy-start(f32[256]{0:T(256)} %param.13) | copy-start | bytes 3076
  13.4 6.1 %copy-start.1 = (s32[8192]{0:T(1024)S(1)}, s32[8192]{0:T(1024)}, u32[]{:S(2)}) copy-start(s32[8192]{0:T(1024)} %param.11) | copy-start | bytes 98308
  13.4 178.0 %all-to-all-start = ((bf16[256,32,256]{2,0,1:T(8,128)(2,1)}), bf16[256,32,256]{2,0,1:T(8,128)(2,1)}, u32[]{:S(2)}, u32[]{:S(2)}) async-start(bf16[256,32,256]{2,0,1:T(8,128)(2,1)} %copy.20), calls=%async_computation | async-start | bytes 8388608 | tf_op jit(solution)/shard_map/all_to_all | solution.py:53
  19.5 112.0 %copy-start.2 = (f32[8192]{0:T(1024)S(1)}, f32[8192]{0:T(1024)}, u32[]{:S(2)}) copy-start(f32[8192]{0:T(1024)} %param.12) | copy-start | bytes 98308
  131.5 3.6 %copy-start = (bf16[256,8192]{1,0:T(8,128)(2,1)S(1)}, bf16[256,8192]{1,0:T(8,128)(2,1)}, u32[]{:S(2)}) copy-start(bf16[256,8192]{1,0:T(8,128)(2,1)} %param.10) | copy-start | bytes 12582916
  135.1 47.2 %copy-start.5 = (s32[2,128]{1,0:T(2,128)S(1)}, s32[2,128]{1,0:T(2,128)}, u32[]{:S(2)}) copy-start(s32[2,128]{1,0:T(2,128)} %param.15) | copy-start | bytes 3076
  136.0 50.2 %copy-start.3 = (f32[256]{0:T(256)S(1)}, f32[256]{0:T(256)}, u32[]{:S(2)}) copy-start(f32[256]{0:T(256)} %param.14) | copy-start | bytes 3076
  269.2 46.3 %copy-start.4 = (f32[256]{0:T(256)}, f32[256]{0:T(256)S(1)}, u32[]{:S(2)}) copy-start(f32[256]{0:T(256)S(1)} %scatter_custom_fusion.1) | copy-start | bytes 3076
where the time goes:
time: 316 us; the launch traced here: 315 us
  blocking collectives  232 us (73%)
  local copies, waits for them, and re-layouts  32.1 us (10%)
  matrix products  31.5 us (10%)
  other arithmetic  10.4 us (3%)
  starting transfers between devices  6.02 us (2%)
    psum x1, blocking collectives, body(): start_margin = lax.psum(start_part, 'shard')  109 us
    psum x1, blocking collectives, body(): update_two = lax.psum(second_part, 'shard')  42.2 us
    unnamed x1, blocking collectives  42.1 us
    psum x1, blocking collectives, body(): update_one = lax.psum(update_part, 'shard')  38.4 us
    dot_general x32, matrix products, update_group(): jnp.dot(columns, group_label * change, precision=lax.Precision.HIGHEST)  7.97 us
    unnamed x15, local copies, waits for them, and re-layouts  6.44 us
    all_to_all x1, local copies, waits for them, and re-layouts, body(): lax.all_to_all(data_t, 'shard', split_axis=1, concat_axis=0, tiled=True)  6.41 us
  transfers between devices with their start and end apart: 1, of which 0 were waited for; matrix products, arithmetic and copies ran while one was open for 6% of the time, Pallas kernels for 0%

commit v1 on v0

--- a/solution.py
+++ b/solution.py
@@ -89,7 +89,8 @@
     change_two = (own_signs * (alpha_two - alpha_one)).astype(jnp.bfloat16)
     second_part = jnp.dot(relaid, change_two, preferred_element_type=jnp.float32) * (2.0 / devices)
     feat_first = device_index * local_feat
-    update_two = lax.psum(second_part, "shard")
+    parts = lax.all_gather(second_part, "shard")
+    update_two = jnp.sum(parts, axis=0)
     own_two = lax.dynamic_slice_in_dim(update_two, feat_first, local_feat)
     own_one = lax.dynamic_slice_in_dim(update_one, feat_first, local_feat)
     return (primal + own_one + own_two, alpha_two, objective)

time: 316 us -> 347 us (1.098)
  waiting for transfers between devices: 0.01 us -> 54.5 us
  blocking collectives: 232 us -> 190 us
  between operations: 2.28 us -> 15.7 us
    all_gather x0 -> x1, waiting for transfers between devices: none -> 54.5 us  [body(): parts = lax.all_gather(second_part, 'shard')]
    psum x1 -> x0, blocking collectives: 42.2 us -> none  [body(): update_two = lax.psum(second_part, 'shard')]
  transfers between devices with their start and end apart: 1 -> 2, of which waited for: 0 -> 1; matrix products, arithmetic and copies ran while one was open for 6% -> 6% of each run, Pallas kernels for 0% -> 0%
where the time goes in v1:
time: 347 us; the launch traced here: 344 us
  blocking collectives  190 us (55%)
  waiting for transfers between devices  54.5 us (16%)
  local copies, waits for them, and re-layouts  33.7 us (10%)
  matrix products  31.5 us (9%)
  between operations  15.7 us (5%)
  other arithmetic  11.2 us (3%)
  starting transfers between devices  6.06 us (2%)
    psum x1, blocking collectives, body(): start_margin = lax.psum(start_part, 'shard')  109 us
    all_gather x1, waiting for transfers between devices, body(): parts = lax.all_gather(second_part, 'shard')  54.5 us
    unnamed x1, blocking collectives  42.1 us
    psum x1, blocking collectives, body(): update_one = lax.psum(update_part, 'shard')  38.5 us
    dot_general x32, matrix products, update_group(): jnp.dot(columns, group_label * change, precision=lax.Precision.HIGHEST)  7.97 us
  transfers between devices with their start and end apart: 2, of which 1 were waited for; matrix products, arithmetic and copies ran while one was open for 6% of the time, Pallas kernels for 0%

profile of v1, /device:TPU:14, one launch (start us, length us, event | category | flops | bytes accessed | tf_op | source)
XLA Modules:
  0.0 343.6 jit_solution(7898161168368959883)
XLA Ops:
  7.2 6.4 %copy.25 = bf16[256,8192]{0,1:T(8,128)(2,1)} copy(bf16[256,8192]{1,0:T(8,128)(2,1)} %param.10) | data formatting | bytes 8388608 | tf_op args[0]
  13.6 6.4 %copy.26 = bf16[256,32,256]{2,0,1:T(8,128)(2,1)} copy(bf16[256,32,256]{0,2,1:T(8,128)(2,1)} %bitcast.48) | data formatting | bytes 8388608 | tf_op jit(solution)/shard_map/all_to_all | solution.py:53
  20.0 6.0 %all-to-all-start = ((bf16[256,32,256]{2,0,1:T(8,128)(2,1)}), bf16[256,32,256]{2,0,1:T(8,128)(2,1)}, u32[]{:S(2)}, u32[]{:S(2)}) async-start(bf16[256,32,256]{2,0,1:T(8,128)(2,1)} %copy.26), calls=%async_computation | async-start | bytes 8388608 | tf_op jit(solution)/shard_map/all_to_all | solution.py:53
  26.1 2.8 fusion.28
  29.0 109.0 %psum.28 = f32[8192]{0:T(1024)S(1)} all-reduce(f32[8192]{0:T(1024)S(1)} %bitcast.53), channel_id=1, replica_groups=mesh['shard'=32] {'shard'}, use_global_device_ids=true, to_apply=%region_0.0 | all-reduce | flops 8192 | bytes 65536 | tf_op jit(solution)/shard_map/psum | solution.py:55
  138.1 3.5 %fusion.29 = f32[1,256]{1,0:T(1,128)S(1)} fusion(bf16[8192,1]{0,1:T(2,128)(2,1)S(1)} %reshape.138, bf16[256,8192]{1,0:T(8,128)(2,1)} %param.10), kind=kOutput, calls=%fused_computation.58 | convolution fusion | flops 4194304 | bytes 4211712 | tf_op jit(solution)/shard_map/dot_general | solution.py:59
  143.2 2.8 fusion.30
  146.0 42.1 %all-reduce = f32[8192]{0:T(1024)S(1)} all-reduce(f32[8192]{0:T(1024)S(1)} %bitcast.54), channel_id=3, replica_groups=mesh['shard'=32] {'shard'}, use_global_device_ids=true, to_apply=%region_1.2.clone | all-reduce | flops 8192 | bytes 65536
  188.9 1.9 gather_fusion.3
  190.8 1.9 gather_fusion.2
  192.8 1.9 gather_fusion
  194.8 1.9 gather_fusion.1
  198.0 4.7 %fusion.19 = f32[256,256]{1,0:T(8,128)S(1)} fusion(bf16[256,32,256]{2,0,1:T(8,128)(2,1)} %all-to-all-done), kind=kOutput, calls=%fused_computation.35 | convolution fusion | flops 1073741824 | bytes 4456448 | tf_op jit(solution)/shard_map/dot_general | solution.py:73
  205.0 2.4 gather_fusion.6
  207.4 8.5 %while.30 = (s32[]{:T(128)}, f32[256]{0:T(256)S(1)}, f32[256]{0:T(256)S(1)}, f32[256]{0:T(256)S(1)}, f32[256]{0:T(256)S(1)}, /*index=5*/f32[256]{0:T(256)S(1)}, ...) while((s32[]{:T(128)}, f32[256]{0:T(256)S(1)}, f32[256]{0:T(256)S(1)}, ...), condition=%wide.region_3.4_spmd, body=%wide.region_2.3_spmd.sunk | while | flops 49814 | bytes 145567 | solution.py:36
  215.9 1.6 scatter_custom_fusion
  217.5 1.9 gather_fusion.7
  219.5 3.4 fusion.31
  222.8 38.5 %all-reduce.1 = (f32[8192]{0:T(1024)S(1)}, f32[]{:T(128)}) all-reduce(f32[8192]{0:T(1024)S(1)} %broadcast_multiply_fusion.1, f32[]{:T(128)S(6)} %add.171), channel_id=1, replica_groups=mesh['shard'=32] {'shard'}, use_global_device_ids=true, to_apply=%region_5.6 | all-reduce | flops 8193 | bytes 65544 | tf_op jit(solution)/shard_map/psum | solution.py:84
  261.3 2.8 fusion.32
  264.2 2.0 gather_fusion.8
  266.1 8.5 %while.31 = (s32[]{:T(128)}, f32[256]{0:T(256)S(1)}, f32[256]{0:T(256)S(1)}, f32[256]{0:T(256)S(1)}, f32[256]{0:T(256)S(1)}, /*index=5*/f32[256]{0:T(256)S(1)}, ...) while((s32[]{:T(128)}, f32[256]{0:T(256)S(1)}, f32[256]{0:T(256)S(1)}, ...), condition=%wide.region_7.8_spmd, body=%wide.region_6.7_spmd.sunk | while | flops 49814 | bytes 145567 | solution.py:36
  276.1 3.4 fusion.33
  280.1 54.5 %all-gather.3.cloned.1.call-done = f32[262144]{0:T(1024)} async-done(((f32[8192]{0:T(1024)}), f32[262144]{0:T(1024)}) %all-gather.3.cloned.1.call-update) | async-done | bytes 1048592 | tf_op jit(solution)/shard_map/all_gather | solution.py:92
  (211 shorter events, 24.5 us)
Async XLA Ops:
  20.0 6.1 %copy-start.6 = (f32[256]{0:T(256)S(1)}, f32[256]{0:T(256)}, u32[]{:S(2)}) copy-start(f32[256]{0:T(256)} %param.13) | copy-start | bytes 3076
  20.0 6.1 %copy-start.1 = (s32[8192]{0:T(1024)S(1)}, s32[8192]{0:T(1024)}, u32[]{:S(2)}) copy-start(s32[8192]{0:T(1024)} %param.11) | copy-start | bytes 98308
  20.0 178.1 %all-to-all-start = ((bf16[256,32,256]{2,0,1:T(8,128)(2,1)}), bf16[256,32,256]{2,0,1:T(8,128)(2,1)}, u32[]{:S(2)}, u32[]{:S(2)}) async-start(bf16[256,32,256]{2,0,1:T(8,128)(2,1)} %copy.26), calls=%async_computation | async-start | bytes 8388608 | tf_op jit(solution)/shard_map/all_to_all | solution.py:53
  26.0 112.0 %copy-start.2 = (f32[8192]{0:T(1024)S(1)}, f32[8192]{0:T(1024)}, u32[]{:S(2)}) copy-start(f32[8192]{0:T(1024)} %param.12) | copy-start | bytes 98308
  26.0 308.6 %all-gather.3.cloned.1.call-start = ((), (), s32[]{:S(2)}) async-start(), calls=%async_computation.1 | async-start | bytes 1081344 | tf_op jit(solution)/shard_map/all_gather | solution.py:92
  138.0 3.6 %copy-start = (bf16[256,8192]{1,0:T(8,128)(2,1)S(1)}, bf16[256,8192]{1,0:T(8,128)(2,1)}, u32[]{:S(2)}) copy-start(bf16[256,8192]{1,0:T(8,128)(2,1)} %param.10) | copy-start | bytes 12582916
  141.6 47.2 %copy-start.5 = (s32[2,128]{1,0:T(2,128)S(1)}, s32[2,128]{1,0:T(2,128)}, u32[]{:S(2)}) copy-start(s32[2,128]{1,0:T(2,128)} %param.15) | copy-start | bytes 3076
  142.5 50.2 %copy-start.3 = (f32[256]{0:T(256)S(1)}, f32[256]{0:T(256)}, u32[]{:S(2)}) copy-start(f32[256]{0:T(256)} %param.14) | copy-start | bytes 3076
  276.1 60.7 %copy-start.4 = (f32[256]{0:T(256)}, f32[256]{0:T(256)S(1)}, u32[]{:S(2)}) copy-start(f32[256]{0:T(256)S(1)} %scatter_custom_fusion.1) | copy-start | bytes 3076
Sparse Core Ops, SparseCore 0:
  280.2 54.3 all-gather.2
